TPU v7x, 32 devices: a whole 2x2x4 slice. The times are simulated.
32 devices in a mesh: px: 4 (over y, x), py: 8 (over z, core).
Axes of the slice: x: 2, y: 2, z: 4, core: 2. Of those that a mesh axis runs over, the one named last changes fastest.
Arguments:
- white_noise: float32 [2, 64, 256, 256], P(None, 'px', 'py'), may hold values from -6 to 6
- spectrum: float32 [64, 256, 256], P('px', 'py'), may hold values from 0.1 to 2, as said below
- group_table: int32 [3, 8], replicated, may hold values from 0 to 7, each once within a row
Outputs:
- modulus: float32 [2, 64, 256, 256], P(None, 'px', 'py')
- level_one: float32 [2, 32, 128, 128], P(None, 'px', 'py')
- level_two: float32 [2, 16, 64, 64], P(None, 'px', 'py')
- level_three: float32 [2, 8, 32, 32], P(None, 'px', 'py')
Inputs may be any that keep to these rules, and one draw needn't show every extreme that they name: spectrum[j, m, k] equals spectrum[(64 - j) % 64, (256 - m) % 256, (256 - k) % 256]. `group_table`: each row is a permutation of 0 to 7.
All inputs are finite; a program needn't handle non-finite values.
Results may differ from a plain program's by a relative error of at most 0.000088.
Values sent between devices are 32-bit elements; how exact they have to be, the bound alone decides.
A program may use at most 192 MiB of HBM per device.

v0:
```python
import numpy as np
import jax
import jax.numpy as jnp
from jax import lax
from jax.sharding import PartitionSpec as P


def angles_of(length):
    positions = np.arange(length, dtype=np.int64)
    return positions[:, None] * positions[None, :] % length * (2.0 * np.pi / length)


def complex_table(length, direction):
    angles = angles_of(length)
    cos, sin = (np.cos(angles), direction * np.sin(angles))
    table = np.stack([np.stack([cos, sin], 1), np.stack([-sin, cos], 1)], 0)
    return jnp.asarray(table, jnp.float32)


def half_tables(length):
    angles = angles_of(length)[:, : length // 2]
    ahead = np.stack([np.cos(angles), -np.sin(angles)], 1)
    back = 2.0 * ahead
    nyquist = np.where(np.arange(length) % 2 == 0, 1.0, -1.0)
    ahead[:, 1, 0] = nyquist
    back[:, 0, 0] = 1.0
    back[:, 1, 0] = nyquist
    return (jnp.asarray(ahead, jnp.float32), jnp.asarray(back, jnp.float32))


def einsum(pattern, left, right):
    return jnp.einsum(pattern, left, right, precision=lax.Precision.HIGH)


def swap_first(values):
    first = values[:, :, :1]
    turned = jnp.swapaxes(first, 0, 1)
    return jnp.concatenate([turned, values[:, :, 1:]], 2)


def coarsen(values):
    members, size_x, size_y, size_z = values.shape
    blocks = values.reshape(members, size_x // 2, 2, size_y // 2, 2, size_z // 2, 2)
    return blocks.mean(axis=(2, 4, 6))


def on_device(white_noise, spectrum, group_table):
    members, cells_x, cells_y, length_z = white_noise.shape
    size_px, size_py = (lax.axis_size("px"), lax.axis_size("py"))
    length_x, length_y = (cells_x * size_px, cells_y * size_py)
    half_z = length_z // 2
    block_py, block = (half_z // size_py, half_z // size_py // size_px)
    z_ahead, z_back = half_tables(length_z)
    scale = 1.0 / (length_x * length_y * length_z)
    table = jnp.transpose(spectrum, (2, 0, 1))
    last = jnp.broadcast_to(table[half_z : half_z + 1], (size_py, 1, cells_x, cells_y))
    table = jnp.concatenate([table[:half_z].reshape(size_py, block_py, cells_x, cells_y), last], 1)
    table = lax.all_to_all(table, "py", split_axis=0, concat_axis=3, tiled=True)[0]
    last = jnp.broadcast_to(table[block_py:], (size_px, 1, cells_x, length_y))
    table = jnp.concatenate([table[:block_py].reshape(size_px, block, cells_x, length_y), last], 1)
    table = lax.all_to_all(table, "px", split_axis=0, concat_axis=2, tiled=True)[0] * scale
    is_first = (lax.axis_index("px") == 0) & (lax.axis_index("py") == 0)
    other = jnp.where(is_first, table[block:], table[:1])
    tables = jnp.stack([table[:block], jnp.concatenate([other, table[1:block]], 0)], 0)
    values = einsum("fxyz,zck->fckxy", white_noise, z_ahead)
    values = swap_first(values)
    values = lax.all_to_all(values, "py", split_axis=2, concat_axis=4, tiled=True)
    values = einsum("fckxy,cydm->fdkxm", values, complex_table(length_y, -1.0))
    values = lax.all_to_all(values, "px", split_axis=2, concat_axis=3, tiled=True)
    values = einsum("fckxm,cxdj->fdkjm", values, complex_table(length_x, -1.0))
    values = values * tables[:, None]
    values = einsum("fckjm,cjdx->fdkxm", values, complex_table(length_x, 1.0))
    values = lax.all_to_all(values, "px", split_axis=3, concat_axis=2, tiled=True)
    values = einsum("fckxm,cmdy->fdkxy", values, complex_table(length_y, 1.0))
    values = lax.all_to_all(values, "py", split_axis=4, concat_axis=2, tiled=True)
    values = swap_first(values)
    fields = einsum("fckxy,zck->fxyz", values, z_back)
    modulus = jnp.exp(0.5 * fields)
    levels = []
    level = modulus
    for _ in range(3):
        level = coarsen(level)
        levels.append(level)
    pieces = [jnp.reshape(level, (size_py, -1)) for level in levels]
    widths = [piece.shape[1] for piece in pieces]
    joined = jnp.concatenate(pieces, 1)
    spread = lax.all_to_all(joined, "py", split_axis=0, concat_axis=0, tiled=True)
    picked, start = ([], 0)
    for index, width in enumerate(widths):
        part = spread[:, start : start + width]
        picked.append(jnp.take(part, group_table[index], axis=0))
        start += width
    joined = lax.all_to_all(
        jnp.concatenate(picked, 1), "py", split_axis=0, concat_axis=0, tiled=True
    )
    routed, start = ([], 0)
    for level, width in zip(levels, widths):
        routed.append(joined[:, start : start + width].reshape(level.shape))
        start += width
    return (modulus, routed[0], routed[1], routed[2])


def solution(mesh):
    in_specs = (P(None, "px", "py", None), P("px", "py", None), P())
    out_specs = (P(None, "px", "py", None),) * 4
    return jax.shard_map(
        on_device, mesh=mesh, in_specs=in_specs, out_specs=out_specs, check_vma=False
    )
```

profile of v0, /device:TPU:0, one launch (start us, length us, event | category | flops | bytes accessed | tf_op | source)
XLA Modules:
  0.0 335.8 jit_solution(13237479351401507157)
XLA Ops:
  0.7 2.4 copy.69
  3.3 1.2 reshape.221
  4.5 6.4 %all-to-all-start.2 = ((f32[8,1,8704]{2,1,0:T(1,128)}), f32[8,1,8704]{2,1,0:T(1,128)S(1)}, u32[]{:S(2)}, u32[]{:S(2)}) async-start(f32[8,1,8704]{2,1,0:T(1,128)} %reshape.221), calls=%async_computation.2 | async-start | bytes 557056 | tf_op jit(solution)/shard_map/all_to_all | solution.py:58
  12.2 4.4 %copy.62 = f32[2,2,128,16,32]{4,3,0,1,2:T(8,128)} copy(f32[2,2,128,16,32]{2,4,3,0,1:T(8,128)S(1)} %pad_maximum_fusion.1) | data formatting | bytes 2097152 | tf_op jit(solution)/shard_map/concatenate | solution.py:38
  16.6 4.8 %reshape.219 = f32[8,1,32768]{2,1,0:T(1,128)} reshape(f32[128,2,2,16,32]{4,3,2,1,0:T(8,128)} %bitcast.161) | data formatting | bytes 2097152
  21.5 5.1 %all-to-all-start = ((f32[8,1,32768]{2,1,0:T(1,128)}), f32[8,1,32768]{2,1,0:T(1,128)S(1)}, u32[]{:S(2)}, u32[]{:S(2)}) async-start(f32[8,1,32768]{2,1,0:T(1,128)} %reshape.219), calls=%async_computation | async-start | bytes 2097152 | tf_op jit(solution)/shard_map/all_to_all | solution.py:67
  27.1 1.3 reduce.1
  30.7 22.5 %all-to-all-done = f32[8,1,32768]{2,1,0:T(1,128)S(1)} async-done(((f32[8,1,32768]{2,1,0:T(1,128)}), f32[8,1,32768]{2,1,0:T(1,128)S(1)}, u32[]{:S(2)}, u32[]{:S(2)}) %all-to-all-start) | async-done | bytes 1048608 | tf_op jit(solution)/shard_map/all_to_all | solution.py:67
  53.1 4.2 %all-to-all-start.3 = ((f32[4,5,16,256]{3,2,1,0:T(8,128)}), f32[4,5,16,256]{3,2,1,0:T(8,128)S(1)}, u32[]{:S(2)}, u32[]{:S(2)}) async-start(f32[4,5,16,256]{3,2,1,0:T(8,128)} %pad_maximum_fusion.3), calls=%async_computation.3 | async-start | bytes 655360 | tf_op jit(solution)/shard_map/all_to_all | solution.py:61
  57.3 3.1 reduce
  60.5 3.3 reshape.220
  63.8 6.6 %copy.64 = f32[2,2,16,16,8,32]{5,4,3,1,2,0:T(8,128)} copy(f32[2,2,16,16,8,32]{5,3,0,1,2,4:T(8,128)} %bitcast.162) | data formatting | bytes 2097152 | tf_op jit(solution)/shard_map/all_to_all | solution.py:67
  70.4 3.4 %reshape.204 = f32[2,2,16,16,256,1]{4,3,1,2,0,5:T(8,128)S(1)} reshape(f32[2,2,16,16,8,32]{5,4,3,1,2,0:T(8,128)} %copy.64) | data formatting | bytes 2097152 | tf_op jit(solution)/shard_map/all_to_all | solution.py:67
  76.0 4.3 %all-to-all-start.1 = ((f32[2,2,16,16,256]{4,3,1,0,2:T(8,128)}), f32[2,2,16,16,256]{4,3,1,0,2:T(8,128)S(1)}, u32[]{:S(2)}, u32[]{:S(2)}) async-start(f32[2,2,16,16,256]{4,3,1,0,2:T(8,128)} %copy.65), calls=%async_computation.1 | async-start | bytes 2097152 | tf_op jit(solution)/shard_map/all_to_all | solution.py:69
  80.5 12.5 %all-to-all-done.1 = f32[2,2,16,16,256]{4,3,1,0,2:T(8,128)S(1)} async-done(((f32[2,2,16,16,256]{4,3,1,0,2:T(8,128)}), f32[2,2,16,16,256]{4,3,1,0,2:T(8,128)S(1)}, u32[]{:S(2)}, u32[]{:S(2)}) %all-to-all-start.1) | async-done | bytes 1048608 | tf_op jit(solution)/shard_map/all_to_all | solution.py:69
  95.3 16.1 %all_to_all.120 = f32[2,2,4,64,256]{4,1,2,0,3:T(2,128)S(1)} all-to-all(f32[2,2,4,64,256]{4,1,2,0,3:T(2,128)S(1)} %copy.74), channel_id=1, replica_groups=mesh['px'=4,'py'=8] {'px'}, dimensions={3} | all-to-all | bytes 2097152 | tf_op jit(solution)/shard_map/all_to_all | solution.py:73
  113.0 8.7 %copy.76 = f32[2,2,16,16,256]{3,1,2,0,4:T(2,128)} copy(f32[2,2,16,16,256]{4,3,1,2,0:T(8,128)S(1)} %convolution_bitcast_fusion.1) | data formatting | bytes 2097152 | tf_op jit(solution)/shard_map/fckxm,cmdy->fdkxy/transpose | solution.py:32
  121.7 13.6 %reshape.223 = f32[8,1,32768]{2,1,0:T(1,128)} reshape(f32[256,2,16,2,16]{4,3,2,1,0:T(2,128)} %bitcast.157) | data formatting | bytes 2097152
  135.3 3.7 %all-to-all-start.5 = ((f32[8,1,32768]{2,1,0:T(1,128)}), f32[8,1,32768]{2,1,0:T(1,128)S(1)}, u32[]{:S(2)}, u32[]{:S(2)}) async-start(f32[8,1,32768]{2,1,0:T(1,128)} %reshape.223), calls=%async_computation.5 | async-start | bytes 2097152 | tf_op jit(solution)/shard_map/all_to_all | solution.py:75
  139.0 26.4 %all-to-all-done.5 = f32[8,1,32768]{2,1,0:T(1,128)S(1)} async-done(((f32[8,1,32768]{2,1,0:T(1,128)}), f32[8,1,32768]{2,1,0:T(1,128)S(1)}, u32[]{:S(2)}, u32[]{:S(2)}) %all-to-all-start.5) | async-done | bytes 1048608 | tf_op jit(solution)/shard_map/all_to_all | solution.py:75
  165.5 3.1 reduce.2
  168.6 14.2 %reshape.224 = f32[256,2,16,2,16]{4,3,2,1,0:T(2,128)} reshape(f32[8,32768]{1,0:T(8,128)S(1)} %reduce.2) | data formatting | bytes 2097152
  182.9 12.9 %copy.77 = f32[2,2,16,16,8,32]{5,3,2,4,1,0:T(8,128)} copy(f32[2,2,16,16,8,32]{3,1,2,0,5,4:T(2,128)} %bitcast.158) | data formatting | bytes 2097152 | tf_op jit(solution)/shard_map/all_to_all | solution.py:75
  195.8 4.4 %slice.116 = f32[2,2,127,16,32]{4,3,2,1,0:T(8,128)} slice(f32[2,2,128,16,32]{4,3,2,1,0:T(8,128)} %bitcast.159), slice={[0:2], [0:2], [1:128], [0:16], [0:32]} | slice | bytes 2080768 | tf_op jit(solution)/shard_map/slice | solution.py:38
  201.0 3.8 %copy.104 = f32[2,2,127,16,32]{2,4,1,3,0:T(8,128)S(1)} copy(f32[2,2,127,16,32]{4,3,2,1,0:T(8,128)} %slice.116) | data formatting | bytes 2080768
  206.0 68.4 %reshape.174 = f32[2,8,2,16,2,128,2]{6,5,4,3,2,1,0:T(8,128)} reshape(f32[2,16,32,256]{3,2,1,0:T(8,128)S(1)} %fusion.3) | data formatting | bytes 2097152 | tf_op jit(solution)/shard_map/reshape | solution.py:43
  274.3 20.8 %reduce_sum.27 = f32[2,8,16,128]{3,2,1,0:T(8,128)S(1)} reduce(f32[2,8,2,16,2,128,2]{6,5,4,3,2,1,0:T(8,128)} %reshape.174, f32[]{:T(128)} %constant.71.clone.1), dimensions={2,4,6}, to_apply=%region_0.1 | reduce | flops 229376 | bytes 1179652 | tf_op jit(solution)/shard_map/reduce_sum | solution.py:44
  295.1 9.8 %div.31 = f32[2,4,2,8,2,64,2]{6,5,4,3,2,1,0:T(8,128)} reshape(f32[2,8,16,128]{3,2,1,0:T(8,128)S(1)} %broadcast_multiply_fusion) | data formatting | bytes 262144 | tf_op jit(solution)/shard_map/div | solution.py:44
  304.9 4.1 %reduce_sum.28 = f32[2,4,8,64]{3,2,1,0:T(8,128)S(1)} reduce(f32[2,4,2,8,2,64,2]{6,5,4,3,2,1,0:T(8,128)} %div.31, f32[]{:T(128)} %constant.71.clone.1), dimensions={2,4,6}, to_apply=%region_1.2 | reduce | flops 28672 | bytes 147460 | tf_op jit(solution)/shard_map/reduce_sum | solution.py:44
  311.2 3.4 %all-to-all-start.6 = ((f32[8,1,4672]{2,1,0:T(1,128)}), f32[8,1,4672]{2,1,0:T(1,128)S(1)}, u32[]{:S(2)}, u32[]{:S(2)}) async-start(f32[8,1,4672]{2,1,0:T(1,128)} %all_to_all.106), calls=%async_computation.6 | async-start | bytes 303104 | tf_op jit(solution)/shard_map/all_to_all | solution.py:87
  314.6 6.9 %all-to-all-done.6 = f32[8,1,4672]{2,1,0:T(1,128)S(1)} async-done(((f32[8,1,4672]{2,1,0:T(1,128)}), f32[8,1,4672]{2,1,0:T(1,128)S(1)}, u32[]{:S(2)}, u32[]{:S(2)}) %all-to-all-start.6) | async-done | bytes 149536 | tf_op jit(solution)/shard_map/all_to_all | solution.py:87
  323.8 9.7 %all_to_all.121 = f32[8,1,4672]{2,1,0:T(1,128)S(1)} all-to-all(f32[8,1,4672]{2,1,0:T(1,128)S(1)} %copy.80), channel_id=1, replica_groups=mesh['px'=4,'py'=8] {'py'}, dimensions={0} | all-to-all | bytes 299008 | tf_op jit(solution)/shard_map/all_to_all | solution.py:93
  (92 shorter events, 18.7 us)
Async XLA Ops:
  0.6 10.2 %copy-start = (f32[2,16,32,256]{3,2,1,0:T(8,128)S(1)}, f32[2,16,32,256]{3,2,1,0:T(8,128)}, u32[]{:S(2)}) copy-start(f32[2,16,32,256]{3,2,1,0:T(8,128)} %param.9) | copy-start | bytes 3145732
  0.6 10.2 %copy-start.5 = (f32[256,2,128,1,1]{2,0,4,3,1:T(8,128)S(1)}, f32[256,2,128,1,1]{2,0,4,3,1:T(8,128)}, u32[]{:S(2)}) copy-start(f32[256,2,128,1,1]{2,0,4,3,1:T(8,128)} %constant.80) | copy-start | bytes 786436
  4.5 17.0 %all-to-all-start.2 = ((f32[8,1,8704]{2,1,0:T(1,128)}), f32[8,1,8704]{2,1,0:T(1,128)S(1)}, u32[]{:S(2)}, u32[]{:S(2)}) async-start(f32[8,1,8704]{2,1,0:T(1,128)} %reshape.221), calls=%async_computation.2 | async-start | bytes 557056 | tf_op jit(solution)/shard_map/all_to_all | solution.py:58
  21.5 31.7 %all-to-all-start = ((f32[8,1,32768]{2,1,0:T(1,128)}), f32[8,1,32768]{2,1,0:T(1,128)S(1)}, u32[]{:S(2)}, u32[]{:S(2)}) async-start(f32[8,1,32768]{2,1,0:T(1,128)} %reshape.219), calls=%async_computation | async-start | bytes 2097152 | tf_op jit(solution)/shard_map/all_to_all | solution.py:67
  53.1 22.8 %all-to-all-start.3 = ((f32[4,5,16,256]{3,2,1,0:T(8,128)}), f32[4,5,16,256]{3,2,1,0:T(8,128)S(1)}, u32[]{:S(2)}, u32[]{:S(2)}) async-start(f32[4,5,16,256]{3,2,1,0:T(8,128)} %pad_maximum_fusion.3), calls=%async_computation.3 | async-start | bytes 655360 | tf_op jit(solution)/shard_map/all_to_all | solution.py:61
  70.4 3.4 %copy-start.4 = (f32[2,256,2,256,1,1]{3,1,0,2,5,4:T(8,128)S(1)}, f32[2,256,2,256,1,1]{3,1,0,2,5,4:T(8,128)}, u32[]{:S(2)}) copy-start(f32[2,256,2,256,1,1]{3,1,0,2,5,4:T(8,128)} %constant.81) | copy-start | bytes 3145732
  75.9 17.2 %copy-start.8 = (f32[2,64,2,64,1,1]{1,3,0,2,5,4:T(8,128)S(1)}, f32[2,64,2,64,1,1]{1,3,0,2,5,4:T(8,128)}, u32[]{:S(2)}) copy-start(f32[2,64,2,64,1,1]{1,3,0,2,5,4:T(8,128)} %constant.82) | copy-start | bytes 196612
  76.0 17.1 %all-to-all-start.1 = ((f32[2,2,16,16,256]{4,3,1,0,2:T(8,128)}), f32[2,2,16,16,256]{4,3,1,0,2:T(8,128)S(1)}, u32[]{:S(2)}, u32[]{:S(2)}) async-start(f32[2,2,16,16,256]{4,3,1,0,2:T(8,128)} %copy.65), calls=%async_computation.1 | async-start | bytes 2097152 | tf_op jit(solution)/shard_map/all_to_all | solution.py:69
  80.3 13.5 %copy-start.7 = (f32[2,64,2,64,1,1]{1,3,0,2,5,4:T(8,128)S(1)}, f32[2,64,2,64,1,1]{1,3,0,2,5,4:T(8,128)}, u32[]{:S(2)}) copy-start(f32[2,64,2,64,1,1]{1,3,0,2,5,4:T(8,128)} %constant.83) | copy-start | bytes 196612
  93.8 18.2 %copy-start.3 = (f32[2,256,2,256,1,1]{3,1,0,2,5,4:T(8,128)S(1)}, f32[2,256,2,256,1,1]{3,1,0,2,5,4:T(8,128)}, u32[]{:S(2)}) copy-start(f32[2,256,2,256,1,1]{3,1,0,2,5,4:T(8,128)} %constant.84) | copy-start | bytes 3145732
  121.7 17.3 %copy-start.9 = (s32[3,8]{1,0:T(4,128)S(1)}, s32[3,8]{1,0:T(4,128)}, u32[]{:S(2)}) copy-start(s32[3,8]{1,0:T(4,128)} %param.11) | copy-start | bytes 292
  135.3 30.2 %all-to-all-start.5 = ((f32[8,1,32768]{2,1,0:T(1,128)}), f32[8,1,32768]{2,1,0:T(1,128)S(1)}, u32[]{:S(2)}, u32[]{:S(2)}) async-start(f32[8,1,32768]{2,1,0:T(1,128)} %reshape.223), calls=%async_computation.5 | async-start | bytes 2097152 | tf_op jit(solution)/shard_map/all_to_all | solution.py:75
  200.2 5.1 %copy-start.6 = (f32[256,2,128,1,1]{2,0,1,4,3:T(8,128)S(1)}, f32[256,2,128,1,1]{2,0,1,4,3:T(8,128)}, u32[]{:S(2)}) copy-start(f32[256,2,128,1,1]{2,0,1,4,3:T(8,128)} %constant.85) | copy-start | bytes 786436
  206.0 68.4 %copy-start.2 = (f32[2,16,32,256]{3,2,1,0:T(8,128)}, f32[2,16,32,256]{3,2,1,0:T(8,128)S(1)}, u32[]{:S(2)}) copy-start(f32[2,16,32,256]{3,2,1,0:T(8,128)S(1)} %fusion.3) | copy-start | bytes 3145732
  304.9 30.6 %copy-start.1 = (f32[2,16,32,256]{3,2,1,0:T(8,128)S(1)}, f32[2,16,32,256]{3,2,1,0:T(8,128)}, u32[]{:S(2)}) copy-start(f32[2,16,32,256]{3,2,1,0:T(8,128)} %param.9) | copy-start | bytes 3145732
  311.2 10.3 %all-to-all-start.6 = ((f32[8,1,4672]{2,1,0:T(1,128)}), f32[8,1,4672]{2,1,0:T(1,128)S(1)}, u32[]{:S(2)}, u32[]{:S(2)}) async-start(f32[8,1,4672]{2,1,0:T(1,128)} %all_to_all.106), calls=%async_computation.6 | async-start | bytes 303104 | tf_op jit(solution)/shard_map/all_to_all | solution.py:87
where the time goes:
time: 342 us; the launch traced here: 336 us
  local copies, waits for them, and re-layouts  174 us (51%)
  waiting for transfers between devices  68.4 us (20%)
  other arithmetic  34.2 us (10%)
  starting transfers between devices  27.1 us (8%)
  blocking collectives  25.8 us (8%)
  matrix products  4.61 us (1%)
    reshape x1, local copies, waits for them, and re-layouts, coarsen(): values.reshape(members, size_x // 2, 2, size_y // 2, 2, size_z // 2, 2)  68.4 us
    unnamed x31, local copies, waits for them, and re-layouts  44.2 us
    all_to_all x1, waiting for transfers between devices, on_device(): lax.all_to_all(values, 'py', split_axis=4, concat_axis=2, tiled=True)  26.4 us
    reduce_sum x3, other arithmetic, coarsen(): return blocks.mean(axis=(2, 4, 6))  25 us
    all_to_all x1, waiting for transfers between devices, on_device(): lax.all_to_all(values, 'py', split_axis=2, concat_axis=4, tiled=True)  22.5 us
    all_to_all x1, blocking collectives, on_device(): lax.all_to_all(values, 'px', split_axis=3, concat_axis=2, tiled=True)  16.1 us
    all_to_all x1, local copies, waits for them, and re-layouts, on_device(): lax.all_to_all(values, 'py', split_axis=4, concat_axis=2, tiled=True)  12.9 us
    all_to_all x1, waiting for transfers between devices, on_device(): lax.all_to_all(values, 'px', split_axis=2, concat_axis=3, tiled=True)  12.5 us
  transfers between devices with their start and end apart: 6, of which 4 were waited for; matrix products, arithmetic and copies ran while one was open for 10% of the time, Pallas kernels for 0%

commit v1 on v0

--- a/solution.py
+++ b/solution.py
@@ -72,7 +72,10 @@
     values = einsum("fckjm,cjdx->fdkxm", values, complex_table(length_x, 1.0))
     values = lax.all_to_all(values, "px", split_axis=3, concat_axis=2, tiled=True)
     values = einsum("fckxm,cmdy->fdkxy", values, complex_table(length_y, 1.0))
-    values = lax.all_to_all(values, "py", split_axis=4, concat_axis=2, tiled=True)
+    values = jnp.concatenate(
+        lax.all_to_all(jnp.stack(jnp.split(values, lax.axis_size("py"), axis=4)), "py", 0, 0),
+        axis=2,
+    )
     values = swap_first(values)
     fields = einsum("fckxy,zck->fxyz", values, z_back)
     modulus = jnp.exp(0.5 * fields)

time: 342 us -> 298 us (0.87); the launches traced: 336 us -> 297 us
  local copies, waits for them, and re-layouts: 174 us -> 137 us
    unnamed x31 -> x40, local copies, waits for them, and re-layouts: 44.2 us -> 27.4 us
    all_to_all x1 -> x0, local copies, waits for them, and re-layouts: 12.9 us -> none  [on_device(): lax.all_to_all(values, 'py', split_axis=4, concat_axis=2, tiled=True)]
    transpose x3 -> x2, local copies, waits for them, and re-layouts: 10.6 us -> 1.86 us  [einsum(): return jnp.einsum(pattern, left, right, precision=lax.Precision.HIGH)]
    reshape x0 -> x2, local copies, waits for them, and re-layouts: none -> 3.45 us  [on_device(): jnp.concatenate(lax.all_to_all(jnp.stack(jnp.split(values, lax.axis_size(...]
  transfers between devices with their start and end apart: 6 -> 6, of which waited for: 4 -> 4; matrix products, arithmetic and copies ran while one was open for 10% -> 11% of each run, Pallas kernels for 0% -> 0%
where the time goes in v1:
time: 298 us; the launch traced here: 297 us
  local copies, waits for them, and re-layouts  137 us (46%)
  waiting for transfers between devices  68.2 us (23%)
  other arithmetic  34.2 us (11%)
  starting transfers between devices  26.6 us (9%)
  blocking collectives  25.7 us (9%)
  matrix products  4.61 us (2%)
    reshape x1, local copies, waits for them, and re-layouts, coarsen(): values.reshape(members, size_x // 2, 2, size_y // 2, 2, size_z // 2, 2)  68.4 us
    unnamed x40, local copies, waits for them, and re-layouts  27.4 us
    all_to_all x1, waiting for transfers between devices, on_device(): lax.all_to_all(jnp.stack(jnp.split(values, lax.axis_size('py'), axis=4)),...  26.2 us
    reduce_sum x3, other arithmetic, coarsen(): return blocks.mean(axis=(2, 4, 6))  25 us
    all_to_all x1, waiting for transfers between devices, on_device(): lax.all_to_all(values, 'py', split_axis=2, concat_axis=4, tiled=True)  22.4 us
    all_to_all x1, blocking collectives, on_device(): lax.all_to_all(values, 'px', split_axis=3, concat_axis=2, tiled=True)  16.1 us
    all_to_all x1, waiting for transfers between devices, on_device(): lax.all_to_all(values, 'px', split_axis=2, concat_axis=3, tiled=True)  12.6 us
    div x5, local copies, waits for them, and re-layouts, coarsen(): return blocks.mean(axis=(2, 4, 6))  11 us
  transfers between devices with their start and end apart: 6, of which 4 were waited for; matrix products, arithmetic and copies ran while one was open for 11% of the time, Pallas kernels for 0%

profile of v1, /device:TPU:0, one launch (start us, length us, event | category | flops | bytes accessed | tf_op | source)
XLA Modules:
  0.0 297.4 jit_solution(13409496772535651168)
XLA Ops:
  0.7 2.4 copy.67
  3.3 1.2 reshape.229
  4.5 6.4 %all-to-all-start.2 = ((f32[8,1,8704]{2,1,0:T(1,128)}), f32[8,1,8704]{2,1,0:T(1,128)S(1)}, u32[]{:S(2)}, u32[]{:S(2)}) async-start(f32[8,1,8704]{2,1,0:T(1,128)} %reshape.229), calls=%async_computation.2 | async-start | bytes 557056 | tf_op jit(solution)/shard_map/all_to_all | solution.py:58
  12.2 4.4 %copy.60 = f32[2,2,128,16,32]{4,3,0,1,2:T(8,128)} copy(f32[2,2,128,16,32]{2,4,3,0,1:T(8,128)S(1)} %pad_maximum_fusion.1) | data formatting | bytes 2097152 | tf_op jit(solution)/shard_map/concatenate | solution.py:38
  16.6 4.8 %reshape.227 = f32[8,1,32768]{2,1,0:T(1,128)} reshape(f32[128,2,2,16,32]{4,3,2,1,0:T(8,128)} %bitcast.189) | data formatting | bytes 2097152
  21.5 5.1 %all-to-all-start = ((f32[8,1,32768]{2,1,0:T(1,128)}), f32[8,1,32768]{2,1,0:T(1,128)S(1)}, u32[]{:S(2)}, u32[]{:S(2)}) async-start(f32[8,1,32768]{2,1,0:T(1,128)} %reshape.227), calls=%async_computation | async-start | bytes 2097152 | tf_op jit(solution)/shard_map/all_to_all | solution.py:67
  27.1 1.3 reduce.1
  30.7 22.4 %all-to-all-done = f32[8,1,32768]{2,1,0:T(1,128)S(1)} async-done(((f32[8,1,32768]{2,1,0:T(1,128)}), f32[8,1,32768]{2,1,0:T(1,128)S(1)}, u32[]{:S(2)}, u32[]{:S(2)}) %all-to-all-start) | async-done | bytes 1048608 | tf_op jit(solution)/shard_map/all_to_all | solution.py:67
  53.1 3.7 %all-to-all-start.3 = ((f32[4,5,16,256]{3,2,1,0:T(8,128)}), f32[4,5,16,256]{3,2,1,0:T(8,128)S(1)}, u32[]{:S(2)}, u32[]{:S(2)}) async-start(f32[4,5,16,256]{3,2,1,0:T(8,128)} %pad_maximum_fusion.3), calls=%async_computation.3 | async-start | bytes 655360 | tf_op jit(solution)/shard_map/all_to_all | solution.py:61
  56.9 3.1 %reduce = f32[8,32768]{1,0:T(8,128)S(1)} reduce(f32[8,1,32768]{2,1,0:T(1,128)S(1)} %all-to-all-done, f32[]{:T(128)} %broadcast.137), dimensions={1}, to_apply=%all_to_all.76.reduce_sub_computation | reduce | bytes 2097156 | tf_op jit(solution)/shard_map/all_to_all | solution.py:67
  60.0 3.3 %reshape.228 = f32[128,2,2,16,32]{4,3,2,1,0:T(8,128)} reshape(f32[8,32768]{1,0:T(8,128)S(1)} %reduce) | data formatting | bytes 2097152
  63.3 6.6 %copy.62 = f32[2,2,16,16,8,32]{5,4,3,1,2,0:T(8,128)} copy(f32[2,2,16,16,8,32]{5,3,0,1,2,4:T(8,128)} %bitcast.190) | data formatting | bytes 2097152 | tf_op jit(solution)/shard_map/all_to_all | solution.py:67
  69.9 3.4 %reshape.212 = f32[2,2,16,16,256,1]{4,3,1,2,0,5:T(8,128)S(1)} reshape(f32[2,2,16,16,8,32]{5,4,3,1,2,0:T(8,128)} %copy.62) | data formatting | bytes 2097152 | tf_op jit(solution)/shard_map/all_to_all | solution.py:67
  75.5 4.3 %all-to-all-start.1 = ((f32[2,2,16,16,256]{4,3,1,0,2:T(8,128)}), f32[2,2,16,16,256]{4,3,1,0,2:T(8,128)S(1)}, u32[]{:S(2)}, u32[]{:S(2)}) async-start(f32[2,2,16,16,256]{4,3,1,0,2:T(8,128)} %copy.63), calls=%async_computation.1 | async-start | bytes 2097152 | tf_op jit(solution)/shard_map/all_to_all | solution.py:69
  80.0 12.6 %all-to-all-done.1 = f32[2,2,16,16,256]{4,3,1,0,2:T(8,128)S(1)} async-done(((f32[2,2,16,16,256]{4,3,1,0,2:T(8,128)}), f32[2,2,16,16,256]{4,3,1,0,2:T(8,128)S(1)}, u32[]{:S(2)}, u32[]{:S(2)}) %all-to-all-start.1) | async-done | bytes 1048608 | tf_op jit(solution)/shard_map/all_to_all | solution.py:69
  94.8 16.1 %all_to_all.107 = f32[2,2,4,64,256]{4,1,2,0,3:T(2,128)S(1)} all-to-all(f32[2,2,4,64,256]{4,1,2,0,3:T(2,128)S(1)} %copy.72), channel_id=1, replica_groups=mesh['px'=4,'py'=8] {'px'}, dimensions={3} | all-to-all | bytes 2097152 | tf_op jit(solution)/shard_map/all_to_all | solution.py:73
  113.9 1.9 copy-done.2
  115.8 4.8 %reshape.231 = f32[8,1,32768]{2,1,0:T(1,128)} reshape(f32[8,2,16,2,16,32]{5,4,3,2,1,0:T(8,128)} %bitcast.193) | data formatting | bytes 2097152
  120.7 3.8 %all-to-all-start.5 = ((f32[8,1,32768]{2,1,0:T(1,128)}), f32[8,1,32768]{2,1,0:T(1,128)S(1)}, u32[]{:S(2)}, u32[]{:S(2)}) async-start(f32[8,1,32768]{2,1,0:T(1,128)} %reshape.231), calls=%async_computation.5 | async-start | bytes 2097152 | tf_op jit(solution)/shard_map/all_to_all | solution.py:76
  124.5 26.2 %all-to-all-done.5 = f32[8,1,32768]{2,1,0:T(1,128)S(1)} async-done(((f32[8,1,32768]{2,1,0:T(1,128)}), f32[8,1,32768]{2,1,0:T(1,128)S(1)}, u32[]{:S(2)}, u32[]{:S(2)}) %all-to-all-start.5) | async-done | bytes 1048608 | tf_op jit(solution)/shard_map/all_to_all | solution.py:76
  150.7 3.1 %reduce.2 = f32[8,32768]{1,0:T(8,128)S(1)} reduce(f32[8,1,32768]{2,1,0:T(1,128)S(1)} %all-to-all-done.5, f32[]{:T(128)} %broadcast.137), dimensions={1}, to_apply=%all_to_all.92.reduce_sub_computation | reduce | bytes 2097156 | tf_op jit(solution)/shard_map/all_to_all | solution.py:76
  153.9 3.3 %reshape.232 = f32[8,2,16,2,16,32]{5,4,3,2,1,0:T(8,128)} reshape(f32[8,32768]{1,0:T(8,128)S(1)} %reduce.2) | data formatting | bytes 2097152
  157.2 2.9 bitcast_bitcast_fusion
  160.7 2.3 slice.116
  163.0 3.6 %copy.101 = f32[2,2,127,16,32]{2,4,1,3,0:T(8,128)S(1)} copy(f32[2,2,127,16,32]{4,3,2,1,0:T(8,128)} %slice.116) | data formatting | bytes 2080768
  167.9 68.4 %reshape.182 = f32[2,8,2,16,2,128,2]{6,5,4,3,2,1,0:T(8,128)} reshape(f32[2,16,32,256]{3,2,1,0:T(8,128)S(1)} %fusion.3) | data formatting | bytes 2097152 | tf_op jit(solution)/shard_map/reshape | solution.py:43
  236.2 20.8 %reduce_sum.27 = f32[2,8,16,128]{3,2,1,0:T(8,128)S(1)} reduce(f32[2,8,2,16,2,128,2]{6,5,4,3,2,1,0:T(8,128)} %reshape.182, f32[]{:T(128)} %constant.71.clone.1), dimensions={2,4,6}, to_apply=%region_0.1 | reduce | flops 229376 | bytes 1179652 | tf_op jit(solution)/shard_map/reduce_sum | solution.py:44
  257.0 9.8 %div.31 = f32[2,4,2,8,2,64,2]{6,5,4,3,2,1,0:T(8,128)} reshape(f32[2,8,16,128]{3,2,1,0:T(8,128)S(1)} %broadcast_multiply_fusion) | data formatting | bytes 262144 | tf_op jit(solution)/shard_map/div | solution.py:44
  266.8 4.1 %reduce_sum.28 = f32[2,4,8,64]{3,2,1,0:T(8,128)S(1)} reduce(f32[2,4,2,8,2,64,2]{6,5,4,3,2,1,0:T(8,128)} %div.31, f32[]{:T(128)} %constant.71.clone.1), dimensions={2,4,6}, to_apply=%region_1.2 | reduce | flops 28672 | bytes 147460 | tf_op jit(solution)/shard_map/reduce_sum | solution.py:44
  273.1 3.4 %all-to-all-start.6 = ((f32[8,1,4672]{2,1,0:T(1,128)}), f32[8,1,4672]{2,1,0:T(1,128)S(1)}, u32[]{:S(2)}, u32[]{:S(2)}) async-start(f32[8,1,4672]{2,1,0:T(1,128)} %all_to_all.93), calls=%async_computation.6 | async-start | bytes 303104 | tf_op jit(solution)/shard_map/all_to_all | solution.py:90
  276.5 6.9 %all-to-all-done.6 = f32[8,1,4672]{2,1,0:T(1,128)S(1)} async-done(((f32[8,1,4672]{2,1,0:T(1,128)}), f32[8,1,4672]{2,1,0:T(1,128)S(1)}, u32[]{:S(2)}, u32[]{:S(2)}) %all-to-all-start.6) | async-done | bytes 149536 | tf_op jit(solution)/shard_map/all_to_all | solution.py:90
  285.7 9.7 %all_to_all.108 = f32[8,1,4672]{2,1,0:T(1,128)S(1)} all-to-all(f32[8,1,4672]{2,1,0:T(1,128)S(1)} %copy.77), channel_id=1, replica_groups=mesh['px'=4,'py'=8] {'py'}, dimensions={0} | all-to-all | bytes 299008 | tf_op jit(solution)/shard_map/all_to_all | solution.py:96
  (102 shorter events, 19.8 us)
Async XLA Ops:
  0.6 10.2 %copy-start = (f32[2,16,32,256]{3,2,1,0:T(8,128)S(1)}, f32[2,16,32,256]{3,2,1,0:T(8,128)}, u32[]{:S(2)}) copy-start(f32[2,16,32,256]{3,2,1,0:T(8,128)} %param.9) | copy-start | bytes 3145732
  0.6 10.2 %copy-start.6 = (f32[256,2,128,1,1]{2,0,4,3,1:T(8,128)S(1)}, f32[256,2,128,1,1]{2,0,4,3,1:T(8,128)}, u32[]{:S(2)}) copy-start(f32[256,2,128,1,1]{2,0,4,3,1:T(8,128)} %constant.80) | copy-start | bytes 786436
  4.5 17.0 %all-to-all-start.2 = ((f32[8,1,8704]{2,1,0:T(1,128)}), f32[8,1,8704]{2,1,0:T(1,128)S(1)}, u32[]{:S(2)}, u32[]{:S(2)}) async-start(f32[8,1,8704]{2,1,0:T(1,128)} %reshape.229), calls=%async_computation.2 | async-start | bytes 557056 | tf_op jit(solution)/shard_map/all_to_all | solution.py:58
  21.5 31.7 %all-to-all-start = ((f32[8,1,32768]{2,1,0:T(1,128)}), f32[8,1,32768]{2,1,0:T(1,128)S(1)}, u32[]{:S(2)}, u32[]{:S(2)}) async-start(f32[8,1,32768]{2,1,0:T(1,128)} %reshape.227), calls=%async_computation | async-start | bytes 2097152 | tf_op jit(solution)/shard_map/all_to_all | solution.py:67
  53.1 22.3 %all-to-all-start.3 = ((f32[4,5,16,256]{3,2,1,0:T(8,128)}), f32[4,5,16,256]{3,2,1,0:T(8,128)S(1)}, u32[]{:S(2)}, u32[]{:S(2)}) async-start(f32[4,5,16,256]{3,2,1,0:T(8,128)} %pad_maximum_fusion.3), calls=%async_computation.3 | async-start | bytes 655360 | tf_op jit(solution)/shard_map/all_to_all | solution.py:61
  69.9 3.4 %copy-start.5 = (f32[2,256,2,256,1,1]{3,1,0,2,5,4:T(8,128)S(1)}, f32[2,256,2,256,1,1]{3,1,0,2,5,4:T(8,128)}, u32[]{:S(2)}) copy-start(f32[2,256,2,256,1,1]{3,1,0,2,5,4:T(8,128)} %constant.81) | copy-start | bytes 3145732
  75.5 17.3 %copy-start.9 = (f32[2,64,2,64,1,1]{1,3,0,2,5,4:T(8,128)S(1)}, f32[2,64,2,64,1,1]{1,3,0,2,5,4:T(8,128)}, u32[]{:S(2)}) copy-start(f32[2,64,2,64,1,1]{1,3,0,2,5,4:T(8,128)} %constant.82) | copy-start | bytes 196612
  75.5 17.2 %all-to-all-start.1 = ((f32[2,2,16,16,256]{4,3,1,0,2:T(8,128)}), f32[2,2,16,16,256]{4,3,1,0,2:T(8,128)S(1)}, u32[]{:S(2)}, u32[]{:S(2)}) async-start(f32[2,2,16,16,256]{4,3,1,0,2:T(8,128)} %copy.63), calls=%async_computation.1 | async-start | bytes 2097152 | tf_op jit(solution)/shard_map/all_to_all | solution.py:69
  79.8 13.6 %copy-start.8 = (f32[2,64,2,64,1,1]{1,3,0,2,5,4:T(8,128)S(1)}, f32[2,64,2,64,1,1]{1,3,0,2,5,4:T(8,128)}, u32[]{:S(2)}) copy-start(f32[2,64,2,64,1,1]{1,3,0,2,5,4:T(8,128)} %constant.83) | copy-start | bytes 196612
  93.4 18.1 %copy-start.4 = (f32[2,256,2,256,1,1]{3,1,0,2,5,4:T(8,128)S(1)}, f32[2,256,2,256,1,1]{3,1,0,2,5,4:T(8,128)}, u32[]{:S(2)}) copy-start(f32[2,256,2,256,1,1]{3,1,0,2,5,4:T(8,128)} %constant.84) | copy-start | bytes 3145732
  113.7 10.8 %copy-start.10 = (s32[3,8]{1,0:T(4,128)S(1)}, s32[3,8]{1,0:T(4,128)}, u32[]{:S(2)}) copy-start(s32[3,8]{1,0:T(4,128)} %param.11) | copy-start | bytes 292
  113.9 1.9 copy-start.2
  120.7 30.1 %all-to-all-start.5 = ((f32[8,1,32768]{2,1,0:T(1,128)}), f32[8,1,32768]{2,1,0:T(1,128)S(1)}, u32[]{:S(2)}, u32[]{:S(2)}) async-start(f32[8,1,32768]{2,1,0:T(1,128)} %reshape.231), calls=%async_computation.5 | async-start | bytes 2097152 | tf_op jit(solution)/shard_map/all_to_all | solution.py:76
  163.0 4.1 %copy-start.7 = (f32[256,2,128,1,1]{2,0,1,4,3:T(8,128)S(1)}, f32[256,2,128,1,1]{2,0,1,4,3:T(8,128)}, u32[]{:S(2)}) copy-start(f32[256,2,128,1,1]{2,0,1,4,3:T(8,128)} %constant.85) | copy-start | bytes 786436
  167.8 68.4 %copy-start.3 = (f32[2,16,32,256]{3,2,1,0:T(8,128)}, f32[2,16,32,256]{3,2,1,0:T(8,128)S(1)}, u32[]{:S(2)}) copy-start(f32[2,16,32,256]{3,2,1,0:T(8,128)S(1)} %fusion.3) | copy-start | bytes 3145732
  266.8 30.6 %copy-start.1 = (f32[2,16,32,256]{3,2,1,0:T(8,128)S(1)}, f32[2,16,32,256]{3,2,1,0:T(8,128)}, u32[]{:S(2)}) copy-start(f32[2,16,32,256]{3,2,1,0:T(8,128)} %param.9) | copy-start | bytes 3145732
  273.1 10.3 %all-to-all-start.6 = ((f32[8,1,4672]{2,1,0:T(1,128)}), f32[8,1,4672]{2,1,0:T(1,128)S(1)}, u32[]{:S(2)}, u32[]{:S(2)}) async-start(f32[8,1,4672]{2,1,0:T(1,128)} %all_to_all.93), calls=%async_computation.6 | async-start | bytes 303104 | tf_op jit(solution)/shard_map/all_to_all | solution.py:90
